TPU v7x, 32 devices: a whole 2x2x4 slice. The times are simulated.
32 devices in a mesh: modes: 8 (over z, y), cheb: 4 (over x, core).
Axes of the slice: x: 2, y: 2, z: 4, core: 2. Of those that a mesh axis runs over, the one named last changes fastest.
Arguments:
- start: float32 [2, 2, 2048, 256], P(None, None, ('modes', 'cheb')), may hold values from -45 to 45
- forcing: float32 [2, 2, 2048, 256], P(None, None, ('modes', 'cheb')), may hold values from -45 to 45
- taus: float32 [2048, 256, 256], P(('modes', 'cheb')), may hold values from -5 to 5
Outputs:
- solution: float32 [2, 2, 2048, 256], P(None, None, ('modes', 'cheb'))
All inputs are finite; a program needn't handle non-finite values.
Results may differ from a plain program's by a relative error of at most 0.0002.
Values sent between devices are 32-bit elements; how exact they have to be, the bound alone decides.
A program may use at most 128 MiB of HBM per device.

v0:
```python
import math
import jax
import jax.numpy as jnp
from jax import lax
from jax.sharding import PartitionSpec as P

NEWTON = 2
KRYLOV = 3
HIGH = lax.Precision.HIGHEST
STRENGTH = 0.1


def cheb_rows(degree_count):
    degree = jnp.arange(degree_count, dtype=jnp.int32)[:, None]
    node = 2 * jnp.arange(degree_count, dtype=jnp.int32)[None, :] + 1
    turns = degree * node % (4 * degree_count)
    return jnp.cos(2.0 * math.pi / (4 * degree_count) * turns.astype(jnp.float32))


def phase_table(row_count, col_count, period):
    row_index = jnp.arange(row_count, dtype=jnp.int32)[:, None]
    col_index = jnp.arange(col_count, dtype=jnp.int32)[None, :]
    turns = row_index * col_index % period
    angle = 2.0 * math.pi / period * turns.astype(jnp.float32)
    return (jnp.cos(angle), jnp.sin(angle))


def inverse_points(spectrum, outer_len, inner_len, factor):
    half_inner = inner_len // 2
    lead_shape = spectrum.shape[:-3]
    row_count = spectrum.shape[-2]
    weights = jnp.where(jnp.arange(outer_len * half_inner) == 0, 1.0, 2.0).astype(jnp.float32)
    real_part = (spectrum[..., 0, :, :] * weights).reshape(
        lead_shape + (row_count, half_inner, outer_len)
    )
    imag_part = (spectrum[..., 1, :, :] * weights).reshape(
        lead_shape + (row_count, half_inner, outer_len)
    )
    section_cos, section_sin = phase_table(inner_len, half_inner, inner_len)
    upper_real = jnp.einsum(
        "jq,...yqa->...yja", section_cos, real_part, precision=HIGH
    ) - jnp.einsum("jq,...yqa->...yja", section_sin, imag_part, precision=HIGH)
    upper_imag = jnp.einsum(
        "jq,...yqa->...yja", section_sin, real_part, precision=HIGH
    ) + jnp.einsum("jq,...yqa->...yja", section_cos, imag_part, precision=HIGH)
    twist_cos, twist_sin = phase_table(inner_len, outer_len, inner_len * outer_len)
    turned_real = upper_real * twist_cos - upper_imag * twist_sin
    turned_imag = upper_real * twist_sin + upper_imag * twist_cos
    final_cos, final_sin = phase_table(outer_len, outer_len, outer_len)
    points = jnp.einsum("ta,...yja->...ytj", final_cos, turned_real, precision=HIGH) - jnp.einsum(
        "ta,...yja->...ytj", final_sin, turned_imag, precision=HIGH
    )
    return points.reshape(lead_shape + (row_count, outer_len * inner_len)) * factor


def forward_modes(points, outer_len, inner_len, factor):
    half_inner = inner_len // 2
    lead_shape = points.shape[:-2]
    row_count = points.shape[-2]
    gridded = points.reshape(lead_shape + (row_count, outer_len, inner_len))
    first_cos, first_sin = phase_table(outer_len, outer_len, outer_len)
    part_real = jnp.einsum("at,...ytj->...yaj", first_cos, gridded, precision=HIGH)
    part_imag = -jnp.einsum("at,...ytj->...yaj", first_sin, gridded, precision=HIGH)
    twist_cos, twist_sin = phase_table(outer_len, inner_len, inner_len * outer_len)
    turned_real = part_real * twist_cos + part_imag * twist_sin
    turned_imag = part_imag * twist_cos - part_real * twist_sin
    last_cos, last_sin = phase_table(half_inner, inner_len, inner_len)
    coef_real = jnp.einsum("qj,...yaj->...yqa", last_cos, turned_real, precision=HIGH) + jnp.einsum(
        "qj,...yaj->...yqa", last_sin, turned_imag, precision=HIGH
    )
    coef_imag = jnp.einsum("qj,...yaj->...yqa", last_cos, turned_imag, precision=HIGH) - jnp.einsum(
        "qj,...yaj->...yqa", last_sin, turned_real, precision=HIGH
    )
    coef_real = coef_real.reshape(lead_shape + (row_count, half_inner * outer_len))
    coef_imag = coef_imag.reshape(lead_shape + (row_count, half_inner * outer_len))
    return jnp.stack([coef_real, coef_imag], axis=-3) * factor


def least_squares(hessen, beta_norm):
    steps_count = len(hessen)
    matrix = [
        [hessen[col_index][:, row_index] for row_index in range(col_index + 2)]
        for col_index in range(steps_count)
    ]
    target = [beta_norm] + [jnp.zeros_like(beta_norm) for row_index in range(steps_count)]
    cosines = []
    sines_list = []
    for col_index in range(steps_count):
        column = matrix[col_index]
        for row_index in range(col_index):
            upper_entry = (
                cosines[row_index] * column[row_index]
                + sines_list[row_index] * column[row_index + 1]
            )
            lower_entry = (
                cosines[row_index] * column[row_index + 1]
                - sines_list[row_index] * column[row_index]
            )
            column[row_index] = upper_entry
            column[row_index + 1] = lower_entry
        radius = jnp.sqrt(
            column[col_index] * column[col_index] + column[col_index + 1] * column[col_index + 1]
        )
        cosines.append(column[col_index] / radius)
        sines_list.append(column[col_index + 1] / radius)
        column[col_index] = radius
        target[col_index + 1] = -sines_list[col_index] * target[col_index]
        target[col_index] = cosines[col_index] * target[col_index]
    solved = [None] * steps_count
    for row_index in reversed(range(steps_count)):
        partial_sum = target[row_index]
        for col_index in range(row_index + 1, steps_count):
            partial_sum = partial_sum - matrix[col_index][row_index] * solved[col_index]
        solved[row_index] = partial_sum / matrix[row_index][row_index]
    return solved


def shards(start, forcing, taus):
    group_size = lax.axis_size(("modes", "cheb"))
    local_modes = start.shape[2]
    degrees = start.shape[3]
    total_modes = local_modes * group_size
    points_count = 2 * total_modes
    outer_len = 2 ** ((points_count.bit_length() - 1) // 2)
    inner_len = points_count // outer_len
    spread = 1.0 / math.sqrt(total_modes * degrees)
    gather_factor = math.sqrt(total_modes * degrees) / points_count
    cheb_table = cheb_rows(degrees)
    offset = lax.axis_index(("modes", "cheb")) * local_modes
    wavenumber = (
        16.0 * (offset + jnp.arange(local_modes, dtype=jnp.int32)).astype(jnp.float32) / total_modes
    )
    tau_keep = (jnp.arange(degrees) < degrees - 2).astype(jnp.float32)
    coef_weights = jnp.where(jnp.arange(degrees) == 0, 1.0, 2.0).astype(jnp.float32) / degrees

    def move_out(stacked):
        return lax.all_to_all(stacked, ("modes", "cheb"), split_axis=3, concat_axis=4, tiled=True)

    def move_back(spectrum):
        return lax.all_to_all(spectrum, ("modes", "cheb"), split_axis=3, concat_axis=2, tiled=True)

    def to_points(coefs):
        values = jnp.einsum("brkn,ni->brik", coefs, cheb_table, precision=HIGH)
        slopes = jnp.stack([-wavenumber * values[:, 1], wavenumber * values[:, 0]], axis=1)
        spectrum = move_out(jnp.stack([values, slopes], axis=0))
        grid_pair = inverse_points(spectrum, outer_len, inner_len, spread)
        return (grid_pair[0], grid_pair[1])

    def to_coefficients(points):
        spectrum = forward_modes(points, outer_len, inner_len, gather_factor)
        slab_vals = move_back(spectrum)
        return jnp.einsum("brik,ni->brkn", slab_vals, cheb_table, precision=HIGH) * coef_weights

    def precondition(coefs):
        return jnp.einsum("kam,brkm->brka", taus, coefs * tau_keep, precision=HIGH)

    iterate = start
    for newton_step in range(NEWTON):
        base_points, base_slopes = to_points(iterate)
        residual = iterate + precondition(
            to_coefficients(STRENGTH * base_points * base_slopes) - forcing
        )
        squared = lax.psum(jnp.sum(residual * residual, axis=(1, 2, 3)), ("modes", "cheb"))
        beta_norm = jnp.sqrt(squared)
        krylov_basis = [-residual / beta_norm[:, None, None, None]]
        hessen = []
        for column in range(KRYLOV):
            probe_points, probe_slopes = to_points(krylov_basis[column])
            product = STRENGTH * (base_points * probe_slopes + probe_points * base_slopes)
            applied = krylov_basis[column] + precondition(to_coefficients(product))
            local_dots = jnp.stack(
                [jnp.sum(vector * applied, axis=(1, 2, 3)) for vector in krylov_basis], axis=1
            )
            local_square = jnp.sum(applied * applied, axis=(1, 2, 3))
            projections, square = lax.psum((local_dots, local_square), ("modes", "cheb"))
            remove_applied = applied
            for index, remove_vector in enumerate(krylov_basis):
                remove_applied = (
                    remove_applied - projections[:, index][:, None, None, None] * remove_vector
                )
            applied = remove_applied
            length = jnp.sqrt(square - jnp.sum(projections * projections, axis=1))
            hessen.append(jnp.concatenate([projections, length[:, None]], axis=1))
            krylov_basis.append(applied / length[:, None, None, None])
        solved = least_squares(hessen, beta_norm)
        for column in range(KRYLOV):
            iterate = iterate + solved[column][:, None, None, None] * krylov_basis[column]
    return iterate


def solution(mesh):
    return jax.shard_map(
        shards,
        mesh=mesh,
        in_specs=(
            P(None, None, ("modes", "cheb"), None),
            P(None, None, ("modes", "cheb"), None),
            P(("modes", "cheb"), None, None),
        ),
        out_specs=P(None, None, ("modes", "cheb"), None),
        check_vma=False,
    )
```

profile of v0, /device:TPU:0, one launch (start us, length us, event | category | flops | bytes accessed | tf_op | source)
XLA Modules:
  0.0 1151.1 jit_solution(514577233461936301)
XLA Ops:
  5.2 7.6 all-to-all-start
  13.3 14.9 %all-to-all-done = f32[32,1,4096]{2,1,0:T(1,128)S(1)} async-done(((f32[32,1,4096]{2,1,0:T(1,128)}), f32[32,1,4096]{2,1,0:T(1,128)S(1)}, u32[]{:S(2)}, u32[]{:S(2)}) %all-to-all-start) | async-done | bytes 524320 | tf_op jit(solution)/shard_map/all_to_all | solution.py:137
  48.1 4.3 copy.577
  52.4 7.9 reshape.338
  63.4 10.5 all-to-all-done.1
  75.2 7.6 reshape.339
  82.9 4.4 copy.769
  89.0 17.4 %fusion.14 = f32[64,2,2,256]{3,2,1,0:T(2,128)S(1)} fusion(f32[64,256,256]{2,1,0:T(8,128)} %param.5, f32[2,2,64,256]{3,2,1,0:T(8,128)S(1)} %fusion.73), kind=kOutput, calls=%fused_computation.14 | convolution fusion | flops 201326592 | bytes 17301504 | tf_op jit(solution)/shard_map/kam,brkm->brka/dot_general | solution.py:155
  106.6 38.5 %psum.98 = f32[2]{0:T(128)S(1)} all-reduce(f32[2]{0:T(128)S(1)} %multiply_reduce_fusion.19), channel_id=1, replica_groups=mesh['modes'=8,'cheb'=4] {'modes','cheb'}, use_global_device_ids=true, to_apply=%region_1.2 | all-reduce | flops 2 | bytes 16 | tf_op jit(solution)/shard_map/psum | solution.py:163
  148.7 19.1 %all_to_all.288 = f32[32,1,4096]{2,1,0:T(1,128)S(1)} all-to-all(f32[32,1,4096]{2,1,0:T(1,128)S(1)} %reshape.340), channel_id=1, replica_groups=mesh['modes'=8,'cheb'=4] {'modes','cheb'}, dimensions={0} | all-to-all | bytes 1048576 | tf_op jit(solution)/shard_map/all_to_all | solution.py:137
  191.7 4.3 copy.594
  196.1 7.2 reshape.342
  203.3 13.5 %all_to_all.289 = f32[32,1,2048]{2,1,0:T(1,128)S(1)} all-to-all(f32[32,1,2048]{2,1,0:T(1,128)S(1)} %reshape.342), channel_id=1, replica_groups=mesh['modes'=8,'cheb'=4] {'modes','cheb'}, dimensions={0} | all-to-all | bytes 524288 | tf_op jit(solution)/shard_map/all_to_all | solution.py:140
  218.0 7.6 reshape.343
  225.7 4.4 copy.771
  231.8 17.4 %fusion.12 = f32[64,2,2,256]{3,2,1,0:T(2,128)S(1)} fusion(f32[64,256,256]{2,1,0:T(8,128)} %param.5, f32[2,2,64,256]{3,2,1,0:T(8,128)S(1)} %fusion.74), kind=kOutput, calls=%fused_computation.12 | convolution fusion | flops 201326592 | bytes 17301504 | tf_op jit(solution)/shard_map/kam,brkm->brka/dot_general | solution.py:155
  249.4 38.6 %all-reduce.5 = (f32[2]{0:T(128)S(1)}, f32[2,1]{0,1:T(1,128)S(1)}) all-reduce(f32[2]{0:T(128)S(1)} %get-tuple-element.22, f32[2,1]{0,1:T(1,128)S(1)} %bitcast.1009), channel_id=1, replica_groups=mesh['modes'=8,'cheb'=4] {'modes','cheb'}, use_global_device_ids=true, to_apply=%region_5.6 | all-reduce | flops 4 | bytes 32 | tf_op jit(solution)/shard_map/psum | solution.py:175
  291.5 19.1 %all_to_all.290 = f32[32,1,4096]{2,1,0:T(1,128)S(1)} all-to-all(f32[32,1,4096]{2,1,0:T(1,128)S(1)} %reshape.344), channel_id=1, replica_groups=mesh['modes'=8,'cheb'=4] {'modes','cheb'}, dimensions={0} | all-to-all | bytes 1048576 | tf_op jit(solution)/shard_map/all_to_all | solution.py:137
  334.6 4.3 copy.611
  338.9 7.2 reshape.346
  346.1 13.5 %all_to_all.291 = f32[32,1,2048]{2,1,0:T(1,128)S(1)} all-to-all(f32[32,1,2048]{2,1,0:T(1,128)S(1)} %reshape.346), channel_id=1, replica_groups=mesh['modes'=8,'cheb'=4] {'modes','cheb'}, dimensions={0} | all-to-all | bytes 524288 | tf_op jit(solution)/shard_map/all_to_all | solution.py:140
  360.9 7.6 reshape.347
  368.5 4.4 copy.773
  374.7 17.4 %fusion.10 = f32[64,2,2,256]{3,2,1,0:T(2,128)S(1)} fusion(f32[64,256,256]{2,1,0:T(8,128)} %param.5, f32[2,2,64,256]{3,2,1,0:T(8,128)S(1)} %fusion.75), kind=kOutput, calls=%fused_computation.10 | convolution fusion | flops 201326592 | bytes 17301504 | tf_op jit(solution)/shard_map/kam,brkm->brka/dot_general | solution.py:155
  392.3 38.6 %all-reduce.4 = (f32[2]{0:T(128)S(1)}, f32[2,2]{0,1:T(2,128)S(1)}) all-reduce(f32[2]{0:T(128)S(1)} %get-tuple-element.19, f32[2,2]{0,1:T(2,128)S(1)} %pad_maximum_fusion.10), channel_id=1, replica_groups=mesh['modes'=8,'cheb'=4] {'modes','cheb'}, use_global_device_ids=true, to_apply=%region_10.11 | all-reduce | flops 6 | bytes 48 | tf_op jit(solution)/shard_map/psum | solution.py:175
  434.5 19.1 %all_to_all.292 = f32[32,1,4096]{2,1,0:T(1,128)S(1)} all-to-all(f32[32,1,4096]{2,1,0:T(1,128)S(1)} %reshape.348), channel_id=1, replica_groups=mesh['modes'=8,'cheb'=4] {'modes','cheb'}, dimensions={0} | all-to-all | bytes 1048576 | tf_op jit(solution)/shard_map/all_to_all | solution.py:137
  477.6 4.3 copy.628
  481.9 7.3 reshape.350
  489.2 13.5 %all_to_all.293 = f32[32,1,2048]{2,1,0:T(1,128)S(1)} all-to-all(f32[32,1,2048]{2,1,0:T(1,128)S(1)} %reshape.350), channel_id=1, replica_groups=mesh['modes'=8,'cheb'=4] {'modes','cheb'}, dimensions={0} | all-to-all | bytes 524288 | tf_op jit(solution)/shard_map/all_to_all | solution.py:140
  503.9 7.6 reshape.351
  511.6 4.4 copy.775
  517.7 17.4 %fusion.8 = f32[64,2,2,256]{3,2,1,0:T(2,128)S(1)} fusion(f32[64,256,256]{2,1,0:T(8,128)} %param.5, f32[2,2,64,256]{3,2,1,0:T(8,128)S(1)} %fusion.76), kind=kOutput, calls=%fused_computation.8 | convolution fusion | flops 201326592 | bytes 17301504 | tf_op jit(solution)/shard_map/kam,brkm->brka/dot_general | solution.py:155
  535.4 38.6 %all-reduce.3 = (f32[2]{0:T(128)S(1)}, f32[2,3]{0,1:T(4,128)S(1)}) all-reduce(f32[2]{0:T(128)S(1)} %get-tuple-element.16, f32[2,3]{0,1:T(4,128)S(1)} %pad_maximum_fusion.8), channel_id=1, replica_groups=mesh['modes'=8,'cheb'=4] {'modes','cheb'}, use_global_device_ids=true, to_apply=%region_17.18 | all-reduce | flops 8 | bytes 64 | tf_op jit(solution)/shard_map/psum | solution.py:175
  578.6 19.1 %all_to_all.294 = f32[32,1,4096]{2,1,0:T(1,128)S(1)} all-to-all(f32[32,1,4096]{2,1,0:T(1,128)S(1)} %reshape.352), channel_id=1, replica_groups=mesh['modes'=8,'cheb'=4] {'modes','cheb'}, dimensions={0} | all-to-all | bytes 1048576 | tf_op jit(solution)/shard_map/all_to_all | solution.py:137
  617.0 4.3 copy.645
  621.4 7.2 reshape.354
  628.6 13.5 %all_to_all.295 = f32[32,1,2048]{2,1,0:T(1,128)S(1)} all-to-all(f32[32,1,2048]{2,1,0:T(1,128)S(1)} %reshape.354), channel_id=1, replica_groups=mesh['modes'=8,'cheb'=4] {'modes','cheb'}, dimensions={0} | all-to-all | bytes 524288 | tf_op jit(solution)/shard_map/all_to_all | solution.py:140
  643.3 7.6 reshape.355
  651.0 4.4 copy.777
  657.1 17.4 %fusion.6 = f32[64,2,2,256]{3,2,1,0:T(2,128)S(1)} fusion(f32[64,256,256]{2,1,0:T(8,128)} %param.5, f32[2,2,64,256]{3,2,1,0:T(8,128)S(1)} %fusion.78), kind=kOutput, calls=%fused_computation.6 | convolution fusion | flops 201326592 | bytes 17301504 | tf_op jit(solution)/shard_map/kam,brkm->brka/dot_general | solution.py:155
  674.7 38.5 %psum.105 = f32[2]{0:T(128)S(1)} all-reduce(f32[2]{0:T(128)S(1)} %multiply_reduce_fusion.9), channel_id=1, replica_groups=mesh['modes'=8,'cheb'=4] {'modes','cheb'}, use_global_device_ids=true, to_apply=%region_20.21 | all-reduce | flops 2 | bytes 16 | tf_op jit(solution)/shard_map/psum | solution.py:163
  716.8 19.1 %all_to_all.296 = f32[32,1,4096]{2,1,0:T(1,128)S(1)} all-to-all(f32[32,1,4096]{2,1,0:T(1,128)S(1)} %reshape.356), channel_id=1, replica_groups=mesh['modes'=8,'cheb'=4] {'modes','cheb'}, dimensions={0} | all-to-all | bytes 1048576 | tf_op jit(solution)/shard_map/all_to_all | solution.py:137
  759.8 4.3 copy.662
  764.2 7.2 reshape.358
  771.4 13.5 %all_to_all.297 = f32[32,1,2048]{2,1,0:T(1,128)S(1)} all-to-all(f32[32,1,2048]{2,1,0:T(1,128)S(1)} %reshape.358), channel_id=1, replica_groups=mesh['modes'=8,'cheb'=4] {'modes','cheb'}, dimensions={0} | all-to-all | bytes 524288 | tf_op jit(solution)/shard_map/all_to_all | solution.py:140
  786.1 7.6 reshape.359
  793.8 4.4 copy.779
  799.9 17.4 %fusion.4 = f32[64,2,2,256]{3,2,1,0:T(2,128)S(1)} fusion(f32[64,256,256]{2,1,0:T(8,128)} %param.5, f32[2,2,64,256]{3,2,1,0:T(8,128)S(1)} %fusion.79), kind=kOutput, calls=%fused_computation.4 | convolution fusion | flops 201326592 | bytes 17301504 | tf_op jit(solution)/shard_map/kam,brkm->brka/dot_general | solution.py:155
  817.5 38.6 %all-reduce.2 = (f32[2]{0:T(128)S(1)}, f32[2,1]{0,1:T(1,128)S(1)}) all-reduce(f32[2]{0:T(128)S(1)} %get-tuple-element.13, f32[2,1]{0,1:T(1,128)S(1)} %bitcast.1010), channel_id=1, replica_groups=mesh['modes'=8,'cheb'=4] {'modes','cheb'}, use_global_device_ids=true, to_apply=%region_24.25 | all-reduce | flops 4 | bytes 32 | tf_op jit(solution)/shard_map/psum | solution.py:175
  859.6 19.1 %all_to_all.298 = f32[32,1,4096]{2,1,0:T(1,128)S(1)} all-to-all(f32[32,1,4096]{2,1,0:T(1,128)S(1)} %reshape.360), channel_id=1, replica_groups=mesh['modes'=8,'cheb'=4] {'modes','cheb'}, dimensions={0} | all-to-all | bytes 1048576 | tf_op jit(solution)/shard_map/all_to_all | solution.py:137
  904.3 4.3 copy.679
  908.6 7.2 reshape.362
  915.8 13.5 %all_to_all.299 = f32[32,1,2048]{2,1,0:T(1,128)S(1)} all-to-all(f32[32,1,2048]{2,1,0:T(1,128)S(1)} %reshape.362), channel_id=1, replica_groups=mesh['modes'=8,'cheb'=4] {'modes','cheb'}, dimensions={0} | all-to-all | bytes 524288 | tf_op jit(solution)/shard_map/all_to_all | solution.py:140
  930.6 7.6 reshape.363
  938.2 4.4 copy.781
  944.4 17.4 %fusion.2 = f32[64,2,2,256]{3,2,1,0:T(2,128)S(1)} fusion(f32[64,256,256]{2,1,0:T(8,128)} %param.5, f32[2,2,64,256]{3,2,1,0:T(8,128)S(1)} %fusion.80), kind=kOutput, calls=%fused_computation.2 | convolution fusion | flops 201326592 | bytes 17301504 | tf_op jit(solution)/shard_map/kam,brkm->brka/dot_general | solution.py:155
  962.0 38.6 %all-reduce.1 = (f32[2]{0:T(128)S(1)}, f32[2,2]{0,1:T(2,128)S(1)}) all-reduce(f32[2]{0:T(128)S(1)} %get-tuple-element.10, f32[2,2]{0,1:T(2,128)S(1)} %pad_maximum_fusion.11), channel_id=1, replica_groups=mesh['modes'=8,'cheb'=4] {'modes','cheb'}, use_global_device_ids=true, to_apply=%region_29.30 | all-reduce | flops 6 | bytes 48 | tf_op jit(solution)/shard_map/psum | solution.py:175
  1006.7 19.3 %all_to_all.300 = f32[32,1,4096]{2,1,0:T(1,128)S(1)} all-to-all(f32[32,1,4096]{2,1,0:T(1,128)} %reshape.364), channel_id=1, replica_groups=mesh['modes'=8,'cheb'=4] {'modes','cheb'}, dimensions={0} | all-to-all | bytes 1048576 | tf_op jit(solution)/shard_map/all_to_all | solution.py:137
  1058.0 7.3 reshape.366
  1065.2 13.5 %all_to_all.301 = f32[32,1,2048]{2,1,0:T(1,128)S(1)} all-to-all(f32[32,1,2048]{2,1,0:T(1,128)S(1)} %reshape.366), channel_id=1, replica_groups=mesh['modes'=8,'cheb'=4] {'modes','cheb'}, dimensions={0} | all-to-all | bytes 524288 | tf_op jit(solution)/shard_map/all_to_all | solution.py:140
  1080.0 7.6 reshape.367
  1087.6 4.4 copy.783
  1093.8 17.4 %fusion = f32[64,2,2,256]{3,2,1,0:T(2,128)S(1)} fusion(f32[64,256,256]{2,1,0:T(8,128)} %param.5, f32[2,2,64,256]{3,2,1,0:T(8,128)S(1)} %fusion.81), kind=kOutput, calls=%fused_computation | convolution fusion | flops 201326592 | bytes 17301504 | tf_op jit(solution)/shard_map/kam,brkm->brka/dot_general | solution.py:155
  1111.4 38.6 %all-reduce = (f32[2]{0:T(128)S(1)}, f32[2,3]{0,1:T(4,128)S(1)}) all-reduce(f32[2]{0:T(128)S(1)} %get-tuple-element.7, f32[2,3]{0,1:T(4,128)S(1)} %pad_maximum_fusion.9), channel_id=1, replica_groups=mesh['modes'=8,'cheb'=4] {'modes','cheb'}, use_global_device_ids=true, to_apply=%region_36.37 | all-reduce | flops 8 | bytes 64 | tf_op jit(solution)/shard_map/psum | solution.py:175
  (316 shorter events, 254.3 us)
Async XLA Ops:
  5.2 23.0 %all-to-all-start = ((f32[32,1,4096]{2,1,0:T(1,128)}), f32[32,1,4096]{2,1,0:T(1,128)S(1)}, u32[]{:S(2)}, u32[]{:S(2)}) async-start(f32[32,1,4096]{2,1,0:T(1,128)} %reshape.336), calls=%async_computation | async-start | bytes 1048576 | tf_op jit(solution)/shard_map/all_to_all | solution.py:137
  42.3 45.0 %copy-start.5 = (f32[2,2,64,256]{3,2,1,0:T(8,128)S(1)}, f32[2,2,64,256]{3,2,1,0:T(8,128)}, u32[]{:S(2)}) copy-start(f32[2,2,64,256]{3,2,1,0:T(8,128)} %param.4) | copy-start | bytes 786436
  52.4 54.0 %copy-start = (f32[2,2,64,256]{3,2,1,0:T(8,128)S(1)}, f32[2,2,64,256]{3,2,1,0:T(8,128)}, u32[]{:S(2)}) copy-start(f32[2,2,64,256]{3,2,1,0:T(8,128)} %param.3) | copy-start | bytes 786436
  60.3 13.7 %all-to-all-start.1 = ((f32[32,1,2048]{2,1,0:T(1,128)}), f32[32,1,2048]{2,1,0:T(1,128)S(1)}, u32[]{:S(2)}, u32[]{:S(2)}) async-start(f32[32,1,2048]{2,1,0:T(1,128)} %reshape.338), calls=%async_computation.1 | async-start | bytes 524288 | tf_op jit(solution)/shard_map/all_to_all | solution.py:140
  431.1 104.0 %copy-start.4 = (f32[2,2,64,256]{3,2,1,0:T(8,128)}, f32[2,2,64,256]{3,2,1,0:T(8,128)S(1)}, u32[]{:S(2)}) copy-start(f32[2,2,64,256]{3,2,1,0:T(8,128)S(1)} %subtract_divide_fusion.2) | copy-start | bytes 786436
  481.9 92.2 %copy-start.1 = (f32[2,2,64,256]{3,2,1,0:T(8,128)S(1)}, f32[2,2,64,256]{3,2,1,0:T(8,128)}, u32[]{:S(2)}) copy-start(f32[2,2,64,256]{3,2,1,0:T(8,128)} %param.3) | copy-start | bytes 786436
  611.3 44.1 %copy-start.6 = (f32[2,2,64,256]{3,2,1,0:T(8,128)S(1)}, f32[2,2,64,256]{3,2,1,0:T(8,128)}, u32[]{:S(2)}) copy-start(f32[2,2,64,256]{3,2,1,0:T(8,128)} %param.4) | copy-start | bytes 786436
  1000.8 38.3 %copy-start.2 = (f32[2,2,64,256]{3,2,1,0:T(8,128)}, f32[2,2,64,256]{3,2,1,0:T(8,128)S(1)}, u32[]{:S(2)}) copy-start(f32[2,2,64,256]{3,2,1,0:T(8,128)S(1)} %subtract_divide_fusion) | copy-start | bytes 786436
  1058.0 53.2 %copy-start.3 = (f32[2,2,64,256]{3,2,1,0:T(8,128)S(1)}, f32[2,2,64,256]{3,2,1,0:T(8,128)}, u32[]{:S(2)}) copy-start(f32[2,2,64,256]{3,2,1,0:T(8,128)} %copy-done.2) | copy-start | bytes 786436
where the time goes:
time: 1160 us; the launch traced here: 1150 us
  blocking collectives  537 us (46%)
  matrix products  312 us (27%)
  local copies, waits for them, and re-layouts  229 us (20%)
  other arithmetic  34.4 us (3%)
  waiting for transfers between devices  25.4 us (2%)
    psum x6, blocking collectives, shards(): lax.psum((local_dots, local_square), ('modes', 'cheb'))  232 us
    dot_general x8, matrix products, precondition(): return jnp.einsum('kam,brkm->brka', taus, coefs * tau_keep, precision=HIGH)  139 us
    unnamed x46, local copies, waits for them, and re-layouts  137 us
    all_to_all x7, blocking collectives, move_out(): lax.all_to_all(stacked, ('modes', 'cheb'), split_axis=3, concat_axis=4, t...  134 us
    all_to_all x7, blocking collectives, move_back(): lax.all_to_all(spectrum, ('modes', 'cheb'), split_axis=3, concat_axis=2,...  94.6 us
    psum x2, blocking collectives, shards(): lax.psum(jnp.sum(residual * residual, axis=(1, 2, 3)), ('modes', 'cheb'))  77.1 us
    all_to_all x8, local copies, waits for them, and re-layouts, move_back(): lax.all_to_all(spectrum, ('modes', 'cheb'), split_axis=3, concat_axis=2,...  35.3 us
    mul x8, local copies, waits for them, and re-layouts, forward_modes(): return jnp.stack([coef_real, coef_imag], axis=-3) * factor  34.5 us
  transfers between devices with their start and end apart: 2, of which 2 were waited for; matrix products, arithmetic and copies ran while one was open for 0% of the time, Pallas kernels for 0%

commit v1 on v0

--- a/solution.py
+++ b/solution.py
@@ -134,7 +134,15 @@
     coef_weights = jnp.where(jnp.arange(degrees) == 0, 1.0, 2.0).astype(jnp.float32) / degrees
 
     def move_out(stacked):
-        return lax.all_to_all(stacked, ("modes", "cheb"), split_axis=3, concat_axis=4, tiled=True)
+        return jnp.concatenate(
+            lax.all_to_all(
+                jnp.stack(jnp.split(stacked, lax.axis_size(("modes", "cheb")), axis=3)),
+                ("modes", "cheb"),
+                0,
+                0,
+            ),
+            axis=4,
+        )
 
     def move_back(spectrum):
         return lax.all_to_all(spectrum, ("modes", "cheb"), split_axis=3, concat_axis=2, tiled=True)

time: 1160 us -> 1540 us (1.33)
  local copies, waits for them, and re-layouts: 229 us -> 553 us
  other arithmetic: 34.4 us -> 81.6 us
    another operation x8 -> x264, local copies, waits for them, and re-layouts: 7.04 us -> 253 us  [move_out(): jnp.stack(jnp.split(stacked, lax.axis_size(('modes', 'cheb')), axis=3))]
    unnamed x46 -> x374, local copies, waits for them, and re-layouts: 137 us -> 208 us
    another operation x0 -> x32, other arithmetic: none -> 50.7 us  [move_out(): jnp.stack(jnp.split(stacked, lax.axis_size(('modes', 'cheb')), axis=3))]
    reshape x0 -> x16, local copies, waits for them, and re-layouts: none -> 16.6 us  [move_out(): jnp.concatenate(lax.all_to_all(jnp.stack(jnp.split(stacked, lax.axis_size...]
where the time goes in v1:
time: 1540 us; the launch traced here: 1530 us
  local copies, waits for them, and re-layouts  553 us (36%)
  blocking collectives  539 us (35%)
  matrix products  311 us (20%)
  other arithmetic  81.6 us (5%)
  waiting for transfers between devices  25.5 us (2%)
    another operation x264, local copies, waits for them, and re-layouts, move_out(): jnp.stack(jnp.split(stacked, lax.axis_size(('modes', 'cheb')), axis=3))  253 us
    psum x6, blocking collectives, shards(): lax.psum((local_dots, local_square), ('modes', 'cheb'))  233 us
    unnamed x374, local copies, waits for them, and re-layouts  208 us
    dot_general x8, matrix products, precondition(): return jnp.einsum('kam,brkm->brka', taus, coefs * tau_keep, precision=HIGH)  139 us
    all_to_all x7, blocking collectives, move_out(): lax.all_to_all(jnp.stack(jnp.split(stacked, lax.axis_size(('modes', 'cheb...  134 us
    all_to_all x7, blocking collectives, move_back(): lax.all_to_all(spectrum, ('modes', 'cheb'), split_axis=3, concat_axis=2,...  95.2 us
    psum x2, blocking collectives, shards(): lax.psum(jnp.sum(residual * residual, axis=(1, 2, 3)), ('modes', 'cheb'))  77.5 us
    another operation x32, other arithmetic, move_out(): jnp.stack(jnp.split(stacked, lax.axis_size(('modes', 'cheb')), axis=3))  50.7 us
  transfers between devices with their start and end apart: 2, of which 2 were waited for; matrix products, arithmetic and copies ran while one was open for 0% of the time, Pallas kernels for 0%

profile of v1, /device:TPU:0, one launch (start us, length us, event | category | flops | bytes accessed | tf_op | source)
XLA Modules:
  0.0 1525.5 jit_solution(14764241050535626817)
XLA Ops:
  48.0 7.5 all-to-all-start
  56.0 15.0 all-to-all-done
  90.6 4.3 copy.1071
  94.9 7.9 reshape.402
  106.2 10.5 all-to-all-done.1
  118.0 7.6 reshape.403
  125.6 4.4 copy.1473
  131.8 17.4 %fusion.14 = f32[64,2,2,256]{3,2,1,0:T(2,128)S(1)} fusion(f32[64,256,256]{2,1,0:T(8,128)} %param.5, f32[2,2,64,256]{3,2,1,0:T(8,128)S(1)} %fusion.73), kind=kOutput, calls=%fused_computation.14 | convolution fusion | flops 201326592 | bytes 17301504 | tf_op jit(solution)/shard_map/kam,brkm->brka/dot_general | solution.py:163
  149.4 38.7 %psum.98 = f32[2]{0:T(128)S(1)} all-reduce(f32[2]{0:T(128)S(1)} %multiply_reduce_fusion.19), channel_id=1, replica_groups=mesh['modes'=8,'cheb'=4] {'modes','cheb'}, use_global_device_ids=true, to_apply=%region_1.2 | all-reduce | flops 2 | bytes 16 | tf_op jit(solution)/shard_map/psum | solution.py:171
  225.6 19.1 %all_to_all.184 = f32[32,1,4096]{2,1,0:T(1,128)S(1)} all-to-all(f32[32,1,4096]{2,1,0:T(1,128)S(1)} %reshape.404), channel_id=1, replica_groups=mesh['modes'=8,'cheb'=4] {'modes','cheb'}, dimensions={0} | all-to-all | bytes 1048576 | tf_op jit(solution)/shard_map/all_to_all | solution.py:138
  268.5 4.3 copy.1118
  272.8 7.2 reshape.406
  280.0 13.5 all_to_all.185
  294.8 7.6 reshape.407
  302.5 4.4 copy.1475
  308.6 17.4 %fusion.12 = f32[64,2,2,256]{3,2,1,0:T(2,128)S(1)} fusion(f32[64,256,256]{2,1,0:T(8,128)} %param.5, f32[2,2,64,256]{3,2,1,0:T(8,128)S(1)} %fusion.74), kind=kOutput, calls=%fused_computation.12 | convolution fusion | flops 201326592 | bytes 17301504 | tf_op jit(solution)/shard_map/kam,brkm->brka/dot_general | solution.py:163
  326.2 38.8 %all-reduce.5 = (f32[2]{0:T(128)S(1)}, f32[2,1]{0,1:T(1,128)S(1)}) all-reduce(f32[2]{0:T(128)S(1)} %get-tuple-element.22, f32[2,1]{0,1:T(1,128)S(1)} %bitcast.1481), channel_id=1, replica_groups=mesh['modes'=8,'cheb'=4] {'modes','cheb'}, use_global_device_ids=true, to_apply=%region_5.6 | all-reduce | flops 4 | bytes 32 | tf_op jit(solution)/shard_map/psum | solution.py:183
  423.7 19.1 %all_to_all.186 = f32[32,1,4096]{2,1,0:T(1,128)S(1)} all-to-all(f32[32,1,4096]{2,1,0:T(1,128)S(1)} %reshape.408), channel_id=1, replica_groups=mesh['modes'=8,'cheb'=4] {'modes','cheb'}, dimensions={0} | all-to-all | bytes 1048576 | tf_op jit(solution)/shard_map/all_to_all | solution.py:138
  468.6 4.3 copy.1165
  472.9 7.2 reshape.410
  480.2 13.6 all_to_all.187
  495.0 7.6 reshape.411
  502.6 4.4 copy.1477
  508.8 17.4 %fusion.10 = f32[64,2,2,256]{3,2,1,0:T(2,128)S(1)} fusion(f32[64,256,256]{2,1,0:T(8,128)} %param.5, f32[2,2,64,256]{3,2,1,0:T(8,128)S(1)} %fusion.75), kind=kOutput, calls=%fused_computation.10 | convolution fusion | flops 201326592 | bytes 17301504 | tf_op jit(solution)/shard_map/kam,brkm->brka/dot_general | solution.py:163
  526.4 39.0 %all-reduce.4 = (f32[2]{0:T(128)S(1)}, f32[2,2]{0,1:T(2,128)S(1)}) all-reduce(f32[2]{0:T(128)S(1)} %get-tuple-element.19, f32[2,2]{0,1:T(2,128)S(1)} %pad_maximum_fusion.10), channel_id=1, replica_groups=mesh['modes'=8,'cheb'=4] {'modes','cheb'}, use_global_device_ids=true, to_apply=%region_10.11 | all-reduce | flops 6 | bytes 48 | tf_op jit(solution)/shard_map/psum | solution.py:183
  623.2 19.1 %all_to_all.188 = f32[32,1,4096]{2,1,0:T(1,128)S(1)} all-to-all(f32[32,1,4096]{2,1,0:T(1,128)S(1)} %reshape.412), channel_id=1, replica_groups=mesh['modes'=8,'cheb'=4] {'modes','cheb'}, dimensions={0} | all-to-all | bytes 1048576 | tf_op jit(solution)/shard_map/all_to_all | solution.py:138
  668.2 4.3 copy.1212
  672.6 7.3 reshape.414
  679.9 13.8 all_to_all.189
  694.9 7.6 reshape.415
  702.5 4.4 copy.1479
  708.7 17.4 %fusion.8 = f32[64,2,2,256]{3,2,1,0:T(2,128)S(1)} fusion(f32[64,256,256]{2,1,0:T(8,128)} %param.5, f32[2,2,64,256]{3,2,1,0:T(8,128)S(1)} %fusion.76), kind=kOutput, calls=%fused_computation.8 | convolution fusion | flops 201326592 | bytes 17301504 | tf_op jit(solution)/shard_map/kam,brkm->brka/dot_general | solution.py:163
  726.3 38.8 %all-reduce.3 = (f32[2]{0:T(128)S(1)}, f32[2,3]{0,1:T(4,128)S(1)}) all-reduce(f32[2]{0:T(128)S(1)} %get-tuple-element.16, f32[2,3]{0,1:T(4,128)S(1)} %pad_maximum_fusion.8), channel_id=1, replica_groups=mesh['modes'=8,'cheb'=4] {'modes','cheb'}, use_global_device_ids=true, to_apply=%region_17.18 | all-reduce | flops 8 | bytes 64 | tf_op jit(solution)/shard_map/psum | solution.py:183
  812.8 19.1 %all_to_all.190 = f32[32,1,4096]{2,1,0:T(1,128)S(1)} all-to-all(f32[32,1,4096]{2,1,0:T(1,128)S(1)} %reshape.416), channel_id=1, replica_groups=mesh['modes'=8,'cheb'=4] {'modes','cheb'}, dimensions={0} | all-to-all | bytes 1048576 | tf_op jit(solution)/shard_map/all_to_all | solution.py:138
  851.1 4.3 copy.1259
  855.4 7.2 reshape.418
  862.6 13.5 all_to_all.191
  877.4 7.6 reshape.419
  885.1 4.4 copy.1481
  891.3 17.4 %fusion.6 = f32[64,2,2,256]{3,2,1,0:T(2,128)S(1)} fusion(f32[64,256,256]{2,1,0:T(8,128)} %param.5, f32[2,2,64,256]{3,2,1,0:T(8,128)S(1)} %fusion.78), kind=kOutput, calls=%fused_computation.6 | convolution fusion | flops 201326592 | bytes 17301504 | tf_op jit(solution)/shard_map/kam,brkm->brka/dot_general | solution.py:163
  908.8 38.7 %psum.105 = f32[2]{0:T(128)S(1)} all-reduce(f32[2]{0:T(128)S(1)} %multiply_reduce_fusion.9), channel_id=1, replica_groups=mesh['modes'=8,'cheb'=4] {'modes','cheb'}, use_global_device_ids=true, to_apply=%region_20.21 | all-reduce | flops 2 | bytes 16 | tf_op jit(solution)/shard_map/psum | solution.py:171
  985.1 19.1 %all_to_all.192 = f32[32,1,4096]{2,1,0:T(1,128)S(1)} all-to-all(f32[32,1,4096]{2,1,0:T(1,128)S(1)} %reshape.420), channel_id=1, replica_groups=mesh['modes'=8,'cheb'=4] {'modes','cheb'}, dimensions={0} | all-to-all | bytes 1048576 | tf_op jit(solution)/shard_map/all_to_all | solution.py:138
  1032.1 7.2 reshape.422
  1039.3 13.6 all_to_all.193
  1054.1 7.6 reshape.423
  1061.8 4.4 copy.1483
  1067.9 17.4 %fusion.4 = f32[64,2,2,256]{3,2,1,0:T(2,128)S(1)} fusion(f32[64,256,256]{2,1,0:T(8,128)} %param.5, f32[2,2,64,256]{3,2,1,0:T(8,128)S(1)} %fusion.79), kind=kOutput, calls=%fused_computation.4 | convolution fusion | flops 201326592 | bytes 17301504 | tf_op jit(solution)/shard_map/kam,brkm->brka/dot_general | solution.py:163
  1085.5 39.0 %all-reduce.2 = (f32[2]{0:T(128)S(1)}, f32[2,1]{0,1:T(1,128)S(1)}) all-reduce(f32[2]{0:T(128)S(1)} %get-tuple-element.13, f32[2,1]{0,1:T(1,128)S(1)} %bitcast.1482), channel_id=1, replica_groups=mesh['modes'=8,'cheb'=4] {'modes','cheb'}, use_global_device_ids=true, to_apply=%region_24.25 | all-reduce | flops 4 | bytes 32 | tf_op jit(solution)/shard_map/psum | solution.py:183
  1183.2 19.1 %all_to_all.194 = f32[32,1,4096]{2,1,0:T(1,128)S(1)} all-to-all(f32[32,1,4096]{2,1,0:T(1,128)S(1)} %reshape.424), channel_id=1, replica_groups=mesh['modes'=8,'cheb'=4] {'modes','cheb'}, dimensions={0} | all-to-all | bytes 1048576 | tf_op jit(solution)/shard_map/all_to_all | solution.py:138
  1228.2 4.3 copy.1353
  1232.5 7.2 reshape.426
  1239.7 13.8 all_to_all.195
  1254.7 7.6 reshape.427
  1262.4 4.4 copy.1485
  1268.5 17.4 %fusion.2 = f32[64,2,2,256]{3,2,1,0:T(2,128)S(1)} fusion(f32[64,256,256]{2,1,0:T(8,128)} %param.5, f32[2,2,64,256]{3,2,1,0:T(8,128)S(1)} %fusion.80), kind=kOutput, calls=%fused_computation.2 | convolution fusion | flops 201326592 | bytes 17301504 | tf_op jit(solution)/shard_map/kam,brkm->brka/dot_general | solution.py:163
  1286.1 38.8 %all-reduce.1 = (f32[2]{0:T(128)S(1)}, f32[2,2]{0,1:T(2,128)S(1)}) all-reduce(f32[2]{0:T(128)S(1)} %get-tuple-element.10, f32[2,2]{0,1:T(2,128)S(1)} %pad_maximum_fusion.11), channel_id=1, replica_groups=mesh['modes'=8,'cheb'=4] {'modes','cheb'}, use_global_device_ids=true, to_apply=%region_29.30 | all-reduce | flops 6 | bytes 48 | tf_op jit(solution)/shard_map/psum | solution.py:183
  1382.7 19.1 %all_to_all.196 = f32[32,1,4096]{2,1,0:T(1,128)S(1)} all-to-all(f32[32,1,4096]{2,1,0:T(1,128)S(1)} %reshape.428), channel_id=1, replica_groups=mesh['modes'=8,'cheb'=4] {'modes','cheb'}, dimensions={0} | all-to-all | bytes 1048576 | tf_op jit(solution)/shard_map/all_to_all | solution.py:138
  1427.8 4.3 copy.1400
  1432.2 7.3 reshape.430
  1439.5 13.5 all_to_all.197
  1454.2 7.6 reshape.431
  1461.9 4.4 copy.1487
  1468.1 17.4 %fusion = f32[64,2,2,256]{3,2,1,0:T(2,128)S(1)} fusion(f32[64,256,256]{2,1,0:T(8,128)} %param.5, f32[2,2,64,256]{3,2,1,0:T(8,128)S(1)} %fusion.81), kind=kOutput, calls=%fused_computation | convolution fusion | flops 201326592 | bytes 17301504 | tf_op jit(solution)/shard_map/kam,brkm->brka/dot_general | solution.py:163
  1485.7 38.6 %all-reduce = (f32[2]{0:T(128)S(1)}, f32[2,3]{0,1:T(4,128)S(1)}) all-reduce(f32[2]{0:T(128)S(1)} %get-tuple-element.7, f32[2,3]{0,1:T(4,128)S(1)} %pad_maximum_fusion.9), channel_id=1, replica_groups=mesh['modes'=8,'cheb'=4] {'modes','cheb'}, use_global_device_ids=true, to_apply=%region_36.37 | all-reduce | flops 8 | bytes 64 | tf_op jit(solution)/shard_map/psum | solution.py:183
  (916 shorter events, 625.0 us)
Async XLA Ops:
  0.0 8.1 copy-start.34
  0.0 8.1 copy-start.4
  0.0 8.1 copy-start.8
  48.0 22.9 %all-to-all-start = ((f32[32,1,4096]{2,1,0:T(1,128)}), f32[32,1,4096]{2,1,0:T(1,128)S(1)}, u32[]{:S(2)}, u32[]{:S(2)}) async-start(f32[32,1,4096]{2,1,0:T(1,128)} %reshape.400), calls=%async_computation | async-start | bytes 1048576 | tf_op jit(solution)/shard_map/all_to_all | solution.py:138
  84.8 45.3 %copy-start.32 = (f32[2,2,64,256]{3,2,1,0:T(8,128)S(1)}, f32[2,2,64,256]{3,2,1,0:T(8,128)}, u32[]{:S(2)}) copy-start(f32[2,2,64,256]{3,2,1,0:T(8,128)} %param.4) | copy-start | bytes 786436
  84.8 45.3 %copy-start.35 = (s32[256]{0:T(256)S(1)}, s32[256]{0:T(256)}, u32[]{:S(2)}) copy-start(s32[256]{0:T(256)} %copy-done.34) | copy-start | bytes 3076
  94.9 54.3 %copy-start.2 = (f32[2,2,64,256]{3,2,1,0:T(8,128)S(1)}, f32[2,2,64,256]{3,2,1,0:T(8,128)}, u32[]{:S(2)}) copy-start(f32[2,2,64,256]{3,2,1,0:T(8,128)} %param.3) | copy-start | bytes 786436
  94.9 94.7 %copy-start.5 = (f32[64]{0:T(128)S(1)}, f32[64]{0:T(128)}, u32[]{:S(2)}) copy-start(f32[64]{0:T(128)} %copy-done.4) | copy-start | bytes 772
  94.9 94.7 %copy-start.9 = (f32[64]{0:T(128)S(1)}, f32[64]{0:T(128)}, u32[]{:S(2)}) copy-start(f32[64]{0:T(128)} %copy-done.8) | copy-start | bytes 772
  102.8 14.0 all-to-all-start.1
  106.2 400.9 %copy-start.39 = (f32[256]{0:T(256)}, f32[256]{0:T(256)S(1)}, u32[]{:S(2)}) copy-start(f32[256]{0:T(256)S(1)} %fusion.1144) | copy-start | bytes 3076
  106.2 400.9 %copy-start.43 = (f32[256]{0:T(256)}, f32[256]{0:T(256)S(1)}, u32[]{:S(2)}) copy-start(f32[256]{0:T(256)S(1)} %compare_convert_fusion) | copy-start | bytes 3076
  188.1 1.5 copy-start.30
  365.0 1.6 copy-start.14
  365.0 1.6 copy-start.26
  565.4 1.7 copy-start.18
  565.5 1.7 copy-start.22
  662.2 44.7 %copy-start.36 = (s32[256]{0:T(256)S(1)}, s32[256]{0:T(256)}, u32[]{:S(2)}) copy-start(s32[256]{0:T(256)} %copy-done.34) | copy-start | bytes 3076
  662.3 44.7 %copy-start.40 = (f32[256]{0:T(256)S(1)}, f32[256]{0:T(256)}, u32[]{:S(2)}) copy-start(f32[256]{0:T(256)} %copy-done.39) | copy-start | bytes 3076
  662.3 44.7 %copy-start.44 = (f32[256]{0:T(256)S(1)}, f32[256]{0:T(256)}, u32[]{:S(2)}) copy-start(f32[256]{0:T(256)} %copy-done.43) | copy-start | bytes 3076
  672.5 92.6 %copy-start.15 = (f32[2,1]{0,1:T(1,128)S(1)}, f32[2,1]{0,1:T(1,128)}, u32[]{:S(2)}) copy-start(f32[2,1]{0,1:T(1,128)} %copy-done.14) | copy-start | bytes 28
  672.5 92.6 %copy-start.27 = (f32[2]{0:T(128)S(1)}, f32[2]{0:T(128)}, u32[]{:S(2)}) copy-start(f32[2]{0:T(128)} %copy-done.26) | copy-start | bytes 28
  672.5 92.6 %copy-start.19 = (f32[2,2]{0,1:T(2,128)S(1)}, f32[2,2]{0,1:T(2,128)}, u32[]{:S(2)}) copy-start(f32[2,2]{0,1:T(2,128)} %copy-done.18) | copy-start | bytes 52
  672.5 92.6 %copy-start.23 = (f32[2]{0:T(128)S(1)}, f32[2]{0:T(128)}, u32[]{:S(2)}) copy-start(f32[2]{0:T(128)} %copy-done.22) | copy-start | bytes 28
  672.5 92.6 %copy-start.31 = (f32[2]{0:T(128)S(1)}, f32[2]{0:T(128)}, u32[]{:S(2)}) copy-start(f32[2]{0:T(128)} %copy-done.30) | copy-start | bytes 28
  672.5 92.7 %copy-start.3 = (f32[2,2,64,256]{3,2,1,0:T(8,128)S(1)}, f32[2,2,64,256]{3,2,1,0:T(8,128)}, u32[]{:S(2)}) copy-start(f32[2,2,64,256]{3,2,1,0:T(8,128)} %param.3) | copy-start | bytes 786436
  679.8 86.9 %copy-start.6 = (f32[64]{0:T(128)S(1)}, f32[64]{0:T(128)}, u32[]{:S(2)}) copy-start(f32[64]{0:T(128)} %copy-done.4) | copy-start | bytes 772
  679.8 86.9 %copy-start.10 = (f32[64]{0:T(128)S(1)}, f32[64]{0:T(128)}, u32[]{:S(2)}) copy-start(f32[64]{0:T(128)} %copy-done.8) | copy-start | bytes 772
  765.4 182.2 %copy-start = (f32[2,2,64,256]{3,2,1,0:T(8,128)}, f32[2,2,64,256]{3,2,1,0:T(8,128)S(1)}, u32[]{:S(2)}) copy-start(f32[2,2,64,256]{3,2,1,0:T(8,128)S(1)} %multiply_add_fusion.9) | copy-start | bytes 786436
  845.3 44.2 %copy-start.33 = (f32[2,2,64,256]{3,2,1,0:T(8,128)S(1)}, f32[2,2,64,256]{3,2,1,0:T(8,128)}, u32[]{:S(2)}) copy-start(f32[2,2,64,256]{3,2,1,0:T(8,128)} %param.4) | copy-start | bytes 786436
  845.3 44.2 %copy-start.37 = (s32[256]{0:T(256)S(1)}, s32[256]{0:T(256)}, u32[]{:S(2)}) copy-start(s32[256]{0:T(256)} %copy-done.34) | copy-start | bytes 3076
  845.3 44.2 %copy-start.41 = (f32[256]{0:T(256)S(1)}, f32[256]{0:T(256)}, u32[]{:S(2)}) copy-start(f32[256]{0:T(256)} %copy-done.39) | copy-start | bytes 3076
  845.3 44.2 %copy-start.45 = (f32[256]{0:T(256)S(1)}, f32[256]{0:T(256)}, u32[]{:S(2)}) copy-start(f32[256]{0:T(256)} %copy-done.43) | copy-start | bytes 3076
  855.4 93.7 %copy-start.7 = (f32[64]{0:T(128)S(1)}, f32[64]{0:T(128)}, u32[]{:S(2)}) copy-start(f32[64]{0:T(128)} %copy-done.4) | copy-start | bytes 772
  855.4 93.7 %copy-start.11 = (f32[64]{0:T(128)S(1)}, f32[64]{0:T(128)}, u32[]{:S(2)}) copy-start(f32[64]{0:T(128)} %copy-done.8) | copy-start | bytes 772
  947.6 1.6 copy-start.28
  1124.5 1.6 copy-start.12
  1124.5 1.6 copy-start.24
  1324.9 1.6 copy-start.16
  1324.9 1.6 copy-start.20
  1421.9 44.4 %copy-start.38 = (s32[256]{0:T(256)S(1)}, s32[256]{0:T(256)}, u32[]{:S(2)}) copy-start(s32[256]{0:T(256)} %copy-done.34) | copy-start | bytes 3076
  1421.9 44.4 %copy-start.42 = (f32[256]{0:T(256)S(1)}, f32[256]{0:T(256)}, u32[]{:S(2)}) copy-start(f32[256]{0:T(256)} %copy-done.39) | copy-start | bytes 3076
  1421.9 44.4 %copy-start.46 = (f32[256]{0:T(256)S(1)}, f32[256]{0:T(256)}, u32[]{:S(2)}) copy-start(f32[256]{0:T(256)} %copy-done.43) | copy-start | bytes 3076
  1432.2 92.2 %copy-start.13 = (f32[2,1]{0,1:T(1,128)S(1)}, f32[2,1]{0,1:T(1,128)}, u32[]{:S(2)}) copy-start(f32[2,1]{0,1:T(1,128)} %copy-done.12) | copy-start | bytes 28
  1432.2 92.2 %copy-start.25 = (f32[2]{0:T(128)S(1)}, f32[2]{0:T(128)}, u32[]{:S(2)}) copy-start(f32[2]{0:T(128)} %copy-done.24) | copy-start | bytes 28
  1432.2 92.2 %copy-start.17 = (f32[2,2]{0,1:T(2,128)S(1)}, f32[2,2]{0,1:T(2,128)}, u32[]{:S(2)}) copy-start(f32[2,2]{0,1:T(2,128)} %copy-done.16) | copy-start | bytes 52
  1432.2 92.2 %copy-start.21 = (f32[2]{0:T(128)S(1)}, f32[2]{0:T(128)}, u32[]{:S(2)}) copy-start(f32[2]{0:T(128)} %copy-done.20) | copy-start | bytes 28
  1432.2 92.2 %copy-start.29 = (f32[2]{0:T(128)S(1)}, f32[2]{0:T(128)}, u32[]{:S(2)}) copy-start(f32[2]{0:T(128)} %copy-done.28) | copy-start | bytes 28
  1432.2 92.3 %copy-start.1 = (f32[2,2,64,256]{3,2,1,0:T(8,128)S(1)}, f32[2,2,64,256]{3,2,1,0:T(8,128)}, u32[]{:S(2)}) copy-start(f32[2,2,64,256]{3,2,1,0:T(8,128)} %copy-done) | copy-start | bytes 786436
